TPU v7x, 16 devices: a 4x2x1 block of a 4x4x8 slice. The times are simulated.
16 devices in a mesh: rep: 2 (over y, z), shard: 8 (over x, core).
Axes of the slice: x: 4, y: 2, z: 1, core: 2. Of those that a mesh axis runs over, the one named last changes fastest.
The devices are a block of a 4x4x8 slice.
Arguments:
- ratings: float32 [8192, 4096], P(('rep', 'shard')), parts along dimension 0
- obs_mask: int32 [8192, 4096], P(('rep', 'shard')), parts along dimension 0
- step_counts: int32 [16, 8], P(('rep', 'shard')), parts along dimension 0
- user_init: float32 [8192, 256], P(('rep', 'shard')), parts along dimension 0
- item_init: float32 [8192, 256], P(('rep', 'shard')), parts along dimension 0
Outputs:
- output 1: float32 [8192, 256], P(('rep', 'shard')), parts along dimension 0
- output 2: float32 [8192, 256], P(('rep', 'shard')), parts along dimension 0
There are 2 independent parts. A program takes and returns all parts, laid end to end along the dimension named above; each array names one.
All inputs are finite; a program needn't handle non-finite values.
Results may differ from a plain program's by a relative error of at most 0.00175092.
Values are sent between devices in bfloat16 or wider.
A program may use at most 768 MiB of HBM per device.

v0:
```python
import math
import jax
import jax.numpy as jnp
from jax import lax
from jax.sharding import PartitionSpec as P

EPOCHS = 2


def solution(mesh):
    group_size = mesh.shape["shard"]
    row_spec = P(("rep", "shard"), None)
    shift_perm = [(source, (source - 1) % group_size) for source in range(group_size)]

    def local_run(ratings, obs_mask, step_counts, user_init, item_init):
        users_dev, rank_dim = user_init.shape
        items_dev = item_init.shape[0]
        step_size = 0.4 * math.sqrt(rank_dim) / (users_dev + rank_dim)
        decay_rate = 0.1 * items_dev / math.sqrt(rank_dim)
        dev_index = lax.axis_index("shard")
        step_row = step_counts[0]

        def sub_epoch(sweep_idx, carry_in):
            user_cur, item_cur = carry_in
            col_id = (dev_index + sweep_idx) % group_size
            rating_blk = lax.dynamic_slice_in_dim(ratings, col_id * items_dev, items_dev, axis=1)
            seen_blk = lax.dynamic_slice_in_dim(obs_mask, col_id * items_dev, items_dev, axis=1) != 0

            def grad_step(step_idx, inner_in):
                user_now, item_now = inner_in
                user_half = user_now.astype(jnp.bfloat16)
                item_half = item_now.astype(jnp.bfloat16)
                approx = jnp.einsum("ur,ir->ui", user_half, item_half, preferred_element_type=jnp.float32)
                err_half = jnp.where(seen_blk, approx - rating_blk, 0.0).astype(jnp.bfloat16)
                grad_user = jnp.einsum("ui,ir->ur", err_half, item_half, preferred_element_type=jnp.float32) + decay_rate * user_now
                grad_item = jnp.einsum("ui,ur->ir", err_half, user_half, preferred_element_type=jnp.float32) + decay_rate * item_now
                return user_now - step_size * grad_user, item_now - step_size * grad_item

            user_new, item_new = lax.fori_loop(0, step_row[col_id], grad_step, (user_cur, item_cur))
            return user_new, lax.ppermute(item_new, "shard", shift_perm)

        return lax.fori_loop(0, EPOCHS * group_size, sub_epoch, (user_init, item_init))

    return jax.shard_map(local_run, mesh=mesh, in_specs=(row_spec,) * 5, out_specs=(row_spec, row_spec), check_vma=False)
```

profile of v0, /device:TPU:112, one launch (start us, length us, event | category | flops | bytes accessed | tf_op | source)
XLA Modules:
  0.0 276.9 jit_solution(17708831307403959756)
XLA Ops:
  2.7 273.2 %while.53 = (s32[]{:T(128)}, f32[512,256]{1,0:T(8,128)S(1)}, f32[512,256]{1,0:T(8,128)S(1)}, s32[]{:T(128)}, s32[8]{0:T(128)}, /*index=5*/f32[512,4096]{1,0:T(8,...) while((s32[]{:T(128)}, f32[512,256]{1,0:T(8,128)S(1)}, ...), condition=%wide.region_3.4_spmd, body=%wide.region_0.3_spmd.sunk | while | flops 405274656 | bytes 14680599 | solution.py:42
  9.0 3.4 %collective-permute-start = (f32[512,256]{1,0:T(8,128)S(1)}, f32[512,256]{1,0:T(8,128)S(1)}, u32[]{:S(2)}, u32[]{:S(2)}) collective-permute-start(f32[512,256]{1,0:T(8,128)S(1)} %get-tuple-element.337), channel_id=1, source_target_pairs={{0,7},{1,0},{2,1},{3,2},{4,3},{5,4},{6,5},{7,6},{8,15},{9,8},{10,9... | collective-permute-start | bytes 1572872 | tf_op jit(solution)/shard_map/while/body/eval_jaxpr/ppermute | solution.py:40
  12.4 6.7 %collective-permute-done = f32[512,256]{1,0:T(8,128)S(1)} collective-permute-done((f32[512,256]{1,0:T(8,128)S(1)}, f32[512,256]{1,0:T(8,128)S(1)}, u32[]{:S(2)}, u32[]{:S(2)}) %collective-permute-start) | collective-permute-done | bytes 524320 | tf_op jit(solution)/shard_map/while/body/eval_jaxpr/ppermute | solution.py:40
  25.4 4.9 %collective-permute-start = (f32[512,256]{1,0:T(8,128)S(1)}, f32[512,256]{1,0:T(8,128)S(1)}, u32[]{:S(2)}, u32[]{:S(2)}) collective-permute-start(f32[512,256]{1,0:T(8,128)S(1)} %get-tuple-element.337), channel_id=1, source_target_pairs={{0,7},{1,0},{2,1},{3,2},{4,3},{5,4},{6,5},{7,6},{8,15},{9,8},{10,9... | collective-permute-start | bytes 1572872 | tf_op jit(solution)/shard_map/while/body/eval_jaxpr/ppermute | solution.py:40
  30.3 6.7 %collective-permute-done = f32[512,256]{1,0:T(8,128)S(1)} collective-permute-done((f32[512,256]{1,0:T(8,128)S(1)}, f32[512,256]{1,0:T(8,128)S(1)}, u32[]{:S(2)}, u32[]{:S(2)}) %collective-permute-start) | collective-permute-done | bytes 524320 | tf_op jit(solution)/shard_map/while/body/eval_jaxpr/ppermute | solution.py:40
  43.4 3.2 %collective-permute-start = (f32[512,256]{1,0:T(8,128)S(1)}, f32[512,256]{1,0:T(8,128)S(1)}, u32[]{:S(2)}, u32[]{:S(2)}) collective-permute-start(f32[512,256]{1,0:T(8,128)S(1)} %get-tuple-element.337), channel_id=1, source_target_pairs={{0,7},{1,0},{2,1},{3,2},{4,3},{5,4},{6,5},{7,6},{8,15},{9,8},{10,9... | collective-permute-start | bytes 1572872 | tf_op jit(solution)/shard_map/while/body/eval_jaxpr/ppermute | solution.py:40
  46.5 6.7 %collective-permute-done = f32[512,256]{1,0:T(8,128)S(1)} collective-permute-done((f32[512,256]{1,0:T(8,128)S(1)}, f32[512,256]{1,0:T(8,128)S(1)}, u32[]{:S(2)}, u32[]{:S(2)}) %collective-permute-start) | collective-permute-done | bytes 524320 | tf_op jit(solution)/shard_map/while/body/eval_jaxpr/ppermute | solution.py:40
  57.2 4.0 %while.54 = (s32[]{:T(128)}, f32[512,256]{1,0:T(8,128)S(1)}, f32[512,256]{1,0:T(8,128)S(1)}, s32[]{:T(128)}, f32[512,512]{1,0:T(8,128)S(1)}, /*index=5*/pred[512,512]{1,0:T(32,128)(4,1)S(1)}, s32[]{:T(128)}) while((s32[]{:T(128)}, f32[512,256]{1,0:T(8,128)S(1)}, f32[512,256]{1,0:T(8,128)S(1)}, s32[]{:T(128)}, f32[512,512]{1,0:T(8,128)S(1)}, ...), condition=%wide.region_2.2_spmd, body=%wide.region_1.1_spmd.sunk | while | flops 405012480 | bytes 8126541 | solution.py:39
  62.8 6.7 %collective-permute-done = f32[512,256]{1,0:T(8,128)S(1)} collective-permute-done((f32[512,256]{1,0:T(8,128)S(1)}, f32[512,256]{1,0:T(8,128)S(1)}, u32[]{:S(2)}, u32[]{:S(2)}) %collective-permute-start) | collective-permute-done | bytes 524320 | tf_op jit(solution)/shard_map/while/body/eval_jaxpr/ppermute | solution.py:40
  73.4 4.0 %while.54 = (s32[]{:T(128)}, f32[512,256]{1,0:T(8,128)S(1)}, f32[512,256]{1,0:T(8,128)S(1)}, s32[]{:T(128)}, f32[512,512]{1,0:T(8,128)S(1)}, /*index=5*/pred[512,512]{1,0:T(32,128)(4,1)S(1)}, s32[]{:T(128)}) while((s32[]{:T(128)}, f32[512,256]{1,0:T(8,128)S(1)}, f32[512,256]{1,0:T(8,128)S(1)}, s32[]{:T(128)}, f32[512,512]{1,0:T(8,128)S(1)}, ...), condition=%wide.region_2.2_spmd, body=%wide.region_1.1_spmd.sunk | while | flops 405012480 | bytes 8126541 | solution.py:39
  79.0 6.7 %collective-permute-done = f32[512,256]{1,0:T(8,128)S(1)} collective-permute-done((f32[512,256]{1,0:T(8,128)S(1)}, f32[512,256]{1,0:T(8,128)S(1)}, u32[]{:S(2)}, u32[]{:S(2)}) %collective-permute-start) | collective-permute-done | bytes 524320 | tf_op jit(solution)/shard_map/while/body/eval_jaxpr/ppermute | solution.py:40
  92.0 4.9 %collective-permute-start = (f32[512,256]{1,0:T(8,128)S(1)}, f32[512,256]{1,0:T(8,128)S(1)}, u32[]{:S(2)}, u32[]{:S(2)}) collective-permute-start(f32[512,256]{1,0:T(8,128)S(1)} %get-tuple-element.337), channel_id=1, source_target_pairs={{0,7},{1,0},{2,1},{3,2},{4,3},{5,4},{6,5},{7,6},{8,15},{9,8},{10,9... | collective-permute-start | bytes 1572872 | tf_op jit(solution)/shard_map/while/body/eval_jaxpr/ppermute | solution.py:40
  96.9 6.7 %collective-permute-done = f32[512,256]{1,0:T(8,128)S(1)} collective-permute-done((f32[512,256]{1,0:T(8,128)S(1)}, f32[512,256]{1,0:T(8,128)S(1)}, u32[]{:S(2)}, u32[]{:S(2)}) %collective-permute-start) | collective-permute-done | bytes 524320 | tf_op jit(solution)/shard_map/while/body/eval_jaxpr/ppermute | solution.py:40
  109.9 4.9 %collective-permute-start = (f32[512,256]{1,0:T(8,128)S(1)}, f32[512,256]{1,0:T(8,128)S(1)}, u32[]{:S(2)}, u32[]{:S(2)}) collective-permute-start(f32[512,256]{1,0:T(8,128)S(1)} %get-tuple-element.337), channel_id=1, source_target_pairs={{0,7},{1,0},{2,1},{3,2},{4,3},{5,4},{6,5},{7,6},{8,15},{9,8},{10,9... | collective-permute-start | bytes 1572872 | tf_op jit(solution)/shard_map/while/body/eval_jaxpr/ppermute | solution.py:40
  114.8 6.7 %collective-permute-done = f32[512,256]{1,0:T(8,128)S(1)} collective-permute-done((f32[512,256]{1,0:T(8,128)S(1)}, f32[512,256]{1,0:T(8,128)S(1)}, u32[]{:S(2)}, u32[]{:S(2)}) %collective-permute-start) | collective-permute-done | bytes 524320 | tf_op jit(solution)/shard_map/while/body/eval_jaxpr/ppermute | solution.py:40
  127.8 4.9 %collective-permute-start = (f32[512,256]{1,0:T(8,128)S(1)}, f32[512,256]{1,0:T(8,128)S(1)}, u32[]{:S(2)}, u32[]{:S(2)}) collective-permute-start(f32[512,256]{1,0:T(8,128)S(1)} %get-tuple-element.337), channel_id=1, source_target_pairs={{0,7},{1,0},{2,1},{3,2},{4,3},{5,4},{6,5},{7,6},{8,15},{9,8},{10,9... | collective-permute-start | bytes 1572872 | tf_op jit(solution)/shard_map/while/body/eval_jaxpr/ppermute | solution.py:40
  132.7 6.7 %collective-permute-done = f32[512,256]{1,0:T(8,128)S(1)} collective-permute-done((f32[512,256]{1,0:T(8,128)S(1)}, f32[512,256]{1,0:T(8,128)S(1)}, u32[]{:S(2)}, u32[]{:S(2)}) %collective-permute-start) | collective-permute-done | bytes 524320 | tf_op jit(solution)/shard_map/while/body/eval_jaxpr/ppermute | solution.py:40
  145.7 3.2 %collective-permute-start = (f32[512,256]{1,0:T(8,128)S(1)}, f32[512,256]{1,0:T(8,128)S(1)}, u32[]{:S(2)}, u32[]{:S(2)}) collective-permute-start(f32[512,256]{1,0:T(8,128)S(1)} %get-tuple-element.337), channel_id=1, source_target_pairs={{0,7},{1,0},{2,1},{3,2},{4,3},{5,4},{6,5},{7,6},{8,15},{9,8},{10,9... | collective-permute-start | bytes 1572872 | tf_op jit(solution)/shard_map/while/body/eval_jaxpr/ppermute | solution.py:40
  148.9 6.7 %collective-permute-done = f32[512,256]{1,0:T(8,128)S(1)} collective-permute-done((f32[512,256]{1,0:T(8,128)S(1)}, f32[512,256]{1,0:T(8,128)S(1)}, u32[]{:S(2)}, u32[]{:S(2)}) %collective-permute-start) | collective-permute-done | bytes 524320 | tf_op jit(solution)/shard_map/while/body/eval_jaxpr/ppermute | solution.py:40
  162.0 4.9 %collective-permute-start = (f32[512,256]{1,0:T(8,128)S(1)}, f32[512,256]{1,0:T(8,128)S(1)}, u32[]{:S(2)}, u32[]{:S(2)}) collective-permute-start(f32[512,256]{1,0:T(8,128)S(1)} %get-tuple-element.337), channel_id=1, source_target_pairs={{0,7},{1,0},{2,1},{3,2},{4,3},{5,4},{6,5},{7,6},{8,15},{9,8},{10,9... | collective-permute-start | bytes 1572872 | tf_op jit(solution)/shard_map/while/body/eval_jaxpr/ppermute | solution.py:40
  166.9 6.7 %collective-permute-done = f32[512,256]{1,0:T(8,128)S(1)} collective-permute-done((f32[512,256]{1,0:T(8,128)S(1)}, f32[512,256]{1,0:T(8,128)S(1)}, u32[]{:S(2)}, u32[]{:S(2)}) %collective-permute-start) | collective-permute-done | bytes 524320 | tf_op jit(solution)/shard_map/while/body/eval_jaxpr/ppermute | solution.py:40
  183.1 6.7 %collective-permute-done = f32[512,256]{1,0:T(8,128)S(1)} collective-permute-done((f32[512,256]{1,0:T(8,128)S(1)}, f32[512,256]{1,0:T(8,128)S(1)}, u32[]{:S(2)}, u32[]{:S(2)}) %collective-permute-start) | collective-permute-done | bytes 524320 | tf_op jit(solution)/shard_map/while/body/eval_jaxpr/ppermute | solution.py:40
  193.8 4.0 %while.54 = (s32[]{:T(128)}, f32[512,256]{1,0:T(8,128)S(1)}, f32[512,256]{1,0:T(8,128)S(1)}, s32[]{:T(128)}, f32[512,512]{1,0:T(8,128)S(1)}, /*index=5*/pred[512,512]{1,0:T(32,128)(4,1)S(1)}, s32[]{:T(128)}) while((s32[]{:T(128)}, f32[512,256]{1,0:T(8,128)S(1)}, f32[512,256]{1,0:T(8,128)S(1)}, s32[]{:T(128)}, f32[512,512]{1,0:T(8,128)S(1)}, ...), condition=%wide.region_2.2_spmd, body=%wide.region_1.1_spmd.sunk | while | flops 405012480 | bytes 8126541 | solution.py:39
  199.3 6.7 %collective-permute-done = f32[512,256]{1,0:T(8,128)S(1)} collective-permute-done((f32[512,256]{1,0:T(8,128)S(1)}, f32[512,256]{1,0:T(8,128)S(1)}, u32[]{:S(2)}, u32[]{:S(2)}) %collective-permute-start) | collective-permute-done | bytes 524320 | tf_op jit(solution)/shard_map/while/body/eval_jaxpr/ppermute | solution.py:40
  210.0 4.0 %while.54 = (s32[]{:T(128)}, f32[512,256]{1,0:T(8,128)S(1)}, f32[512,256]{1,0:T(8,128)S(1)}, s32[]{:T(128)}, f32[512,512]{1,0:T(8,128)S(1)}, /*index=5*/pred[512,512]{1,0:T(32,128)(4,1)S(1)}, s32[]{:T(128)}) while((s32[]{:T(128)}, f32[512,256]{1,0:T(8,128)S(1)}, f32[512,256]{1,0:T(8,128)S(1)}, s32[]{:T(128)}, f32[512,512]{1,0:T(8,128)S(1)}, ...), condition=%wide.region_2.2_spmd, body=%wide.region_1.1_spmd.sunk | while | flops 405012480 | bytes 8126541 | solution.py:39
  215.5 6.7 %collective-permute-done = f32[512,256]{1,0:T(8,128)S(1)} collective-permute-done((f32[512,256]{1,0:T(8,128)S(1)}, f32[512,256]{1,0:T(8,128)S(1)}, u32[]{:S(2)}, u32[]{:S(2)}) %collective-permute-start) | collective-permute-done | bytes 524320 | tf_op jit(solution)/shard_map/while/body/eval_jaxpr/ppermute | solution.py:40
  228.5 4.9 %collective-permute-start = (f32[512,256]{1,0:T(8,128)S(1)}, f32[512,256]{1,0:T(8,128)S(1)}, u32[]{:S(2)}, u32[]{:S(2)}) collective-permute-start(f32[512,256]{1,0:T(8,128)S(1)} %get-tuple-element.337), channel_id=1, source_target_pairs={{0,7},{1,0},{2,1},{3,2},{4,3},{5,4},{6,5},{7,6},{8,15},{9,8},{10,9... | collective-permute-start | bytes 1572872 | tf_op jit(solution)/shard_map/while/body/eval_jaxpr/ppermute | solution.py:40
  233.4 6.7 %collective-permute-done = f32[512,256]{1,0:T(8,128)S(1)} collective-permute-done((f32[512,256]{1,0:T(8,128)S(1)}, f32[512,256]{1,0:T(8,128)S(1)}, u32[]{:S(2)}, u32[]{:S(2)}) %collective-permute-start) | collective-permute-done | bytes 524320 | tf_op jit(solution)/shard_map/while/body/eval_jaxpr/ppermute | solution.py:40
  246.4 4.9 %collective-permute-start = (f32[512,256]{1,0:T(8,128)S(1)}, f32[512,256]{1,0:T(8,128)S(1)}, u32[]{:S(2)}, u32[]{:S(2)}) collective-permute-start(f32[512,256]{1,0:T(8,128)S(1)} %get-tuple-element.337), channel_id=1, source_target_pairs={{0,7},{1,0},{2,1},{3,2},{4,3},{5,4},{6,5},{7,6},{8,15},{9,8},{10,9... | collective-permute-start | bytes 1572872 | tf_op jit(solution)/shard_map/while/body/eval_jaxpr/ppermute | solution.py:40
  251.3 6.7 %collective-permute-done = f32[512,256]{1,0:T(8,128)S(1)} collective-permute-done((f32[512,256]{1,0:T(8,128)S(1)}, f32[512,256]{1,0:T(8,128)S(1)}, u32[]{:S(2)}, u32[]{:S(2)}) %collective-permute-start) | collective-permute-done | bytes 524320 | tf_op jit(solution)/shard_map/while/body/eval_jaxpr/ppermute | solution.py:40
  264.4 4.9 %collective-permute-start = (f32[512,256]{1,0:T(8,128)S(1)}, f32[512,256]{1,0:T(8,128)S(1)}, u32[]{:S(2)}, u32[]{:S(2)}) collective-permute-start(f32[512,256]{1,0:T(8,128)S(1)} %get-tuple-element.337), channel_id=1, source_target_pairs={{0,7},{1,0},{2,1},{3,2},{4,3},{5,4},{6,5},{7,6},{8,15},{9,8},{10,9... | collective-permute-start | bytes 1572872 | tf_op jit(solution)/shard_map/while/body/eval_jaxpr/ppermute | solution.py:40
  269.2 6.7 %collective-permute-done = f32[512,256]{1,0:T(8,128)S(1)} collective-permute-done((f32[512,256]{1,0:T(8,128)S(1)}, f32[512,256]{1,0:T(8,128)S(1)}, u32[]{:S(2)}, u32[]{:S(2)}) %collective-permute-start) | collective-permute-done | bytes 524320 | tf_op jit(solution)/shard_map/while/body/eval_jaxpr/ppermute | solution.py:40
  (167 shorter events, 124.3 us)
Async XLA Ops:
  9.0 10.1 %collective-permute-start = (f32[512,256]{1,0:T(8,128)S(1)}, f32[512,256]{1,0:T(8,128)S(1)}, u32[]{:S(2)}, u32[]{:S(2)}) collective-permute-start(f32[512,256]{1,0:T(8,128)S(1)} %get-tuple-element.337), channel_id=1, source_target_pairs={{0,7},{1,0},{2,1},{3,2},{4,3},{5,4},{6,5},{7,6},{8,15},{9,8},{10,9... | collective-permute-start | bytes 1572872 | tf_op jit(solution)/shard_map/while/body/eval_jaxpr/ppermute | solution.py:40
  25.4 11.6 %collective-permute-start = (f32[512,256]{1,0:T(8,128)S(1)}, f32[512,256]{1,0:T(8,128)S(1)}, u32[]{:S(2)}, u32[]{:S(2)}) collective-permute-start(f32[512,256]{1,0:T(8,128)S(1)} %get-tuple-element.337), channel_id=1, source_target_pairs={{0,7},{1,0},{2,1},{3,2},{4,3},{5,4},{6,5},{7,6},{8,15},{9,8},{10,9... | collective-permute-start | bytes 1572872 | tf_op jit(solution)/shard_map/while/body/eval_jaxpr/ppermute | solution.py:40
  43.4 9.9 %collective-permute-start = (f32[512,256]{1,0:T(8,128)S(1)}, f32[512,256]{1,0:T(8,128)S(1)}, u32[]{:S(2)}, u32[]{:S(2)}) collective-permute-start(f32[512,256]{1,0:T(8,128)S(1)} %get-tuple-element.337), channel_id=1, source_target_pairs={{0,7},{1,0},{2,1},{3,2},{4,3},{5,4},{6,5},{7,6},{8,15},{9,8},{10,9... | collective-permute-start | bytes 1572872 | tf_op jit(solution)/shard_map/while/body/eval_jaxpr/ppermute | solution.py:40
  61.3 8.2 %collective-permute-start = (f32[512,256]{1,0:T(8,128)S(1)}, f32[512,256]{1,0:T(8,128)S(1)}, u32[]{:S(2)}, u32[]{:S(2)}) collective-permute-start(f32[512,256]{1,0:T(8,128)S(1)} %get-tuple-element.337), channel_id=1, source_target_pairs={{0,7},{1,0},{2,1},{3,2},{4,3},{5,4},{6,5},{7,6},{8,15},{9,8},{10,9... | collective-permute-start | bytes 1572872 | tf_op jit(solution)/shard_map/while/body/eval_jaxpr/ppermute | solution.py:40
  77.5 8.2 %collective-permute-start = (f32[512,256]{1,0:T(8,128)S(1)}, f32[512,256]{1,0:T(8,128)S(1)}, u32[]{:S(2)}, u32[]{:S(2)}) collective-permute-start(f32[512,256]{1,0:T(8,128)S(1)} %get-tuple-element.337), channel_id=1, source_target_pairs={{0,7},{1,0},{2,1},{3,2},{4,3},{5,4},{6,5},{7,6},{8,15},{9,8},{10,9... | collective-permute-start | bytes 1572872 | tf_op jit(solution)/shard_map/while/body/eval_jaxpr/ppermute | solution.py:40
  92.0 11.6 %collective-permute-start = (f32[512,256]{1,0:T(8,128)S(1)}, f32[512,256]{1,0:T(8,128)S(1)}, u32[]{:S(2)}, u32[]{:S(2)}) collective-permute-start(f32[512,256]{1,0:T(8,128)S(1)} %get-tuple-element.337), channel_id=1, source_target_pairs={{0,7},{1,0},{2,1},{3,2},{4,3},{5,4},{6,5},{7,6},{8,15},{9,8},{10,9... | collective-permute-start | bytes 1572872 | tf_op jit(solution)/shard_map/while/body/eval_jaxpr/ppermute | solution.py:40
  109.9 11.6 %collective-permute-start = (f32[512,256]{1,0:T(8,128)S(1)}, f32[512,256]{1,0:T(8,128)S(1)}, u32[]{:S(2)}, u32[]{:S(2)}) collective-permute-start(f32[512,256]{1,0:T(8,128)S(1)} %get-tuple-element.337), channel_id=1, source_target_pairs={{0,7},{1,0},{2,1},{3,2},{4,3},{5,4},{6,5},{7,6},{8,15},{9,8},{10,9... | collective-permute-start | bytes 1572872 | tf_op jit(solution)/shard_map/while/body/eval_jaxpr/ppermute | solution.py:40
  127.8 11.6 %collective-permute-start = (f32[512,256]{1,0:T(8,128)S(1)}, f32[512,256]{1,0:T(8,128)S(1)}, u32[]{:S(2)}, u32[]{:S(2)}) collective-permute-start(f32[512,256]{1,0:T(8,128)S(1)} %get-tuple-element.337), channel_id=1, source_target_pairs={{0,7},{1,0},{2,1},{3,2},{4,3},{5,4},{6,5},{7,6},{8,15},{9,8},{10,9... | collective-permute-start | bytes 1572872 | tf_op jit(solution)/shard_map/while/body/eval_jaxpr/ppermute | solution.py:40
  145.7 9.9 %collective-permute-start = (f32[512,256]{1,0:T(8,128)S(1)}, f32[512,256]{1,0:T(8,128)S(1)}, u32[]{:S(2)}, u32[]{:S(2)}) collective-permute-start(f32[512,256]{1,0:T(8,128)S(1)} %get-tuple-element.337), channel_id=1, source_target_pairs={{0,7},{1,0},{2,1},{3,2},{4,3},{5,4},{6,5},{7,6},{8,15},{9,8},{10,9... | collective-permute-start | bytes 1572872 | tf_op jit(solution)/shard_map/while/body/eval_jaxpr/ppermute | solution.py:40
  162.0 11.6 %collective-permute-start = (f32[512,256]{1,0:T(8,128)S(1)}, f32[512,256]{1,0:T(8,128)S(1)}, u32[]{:S(2)}, u32[]{:S(2)}) collective-permute-start(f32[512,256]{1,0:T(8,128)S(1)} %get-tuple-element.337), channel_id=1, source_target_pairs={{0,7},{1,0},{2,1},{3,2},{4,3},{5,4},{6,5},{7,6},{8,15},{9,8},{10,9... | collective-permute-start | bytes 1572872 | tf_op jit(solution)/shard_map/while/body/eval_jaxpr/ppermute | solution.py:40
  179.9 9.9 %collective-permute-start = (f32[512,256]{1,0:T(8,128)S(1)}, f32[512,256]{1,0:T(8,128)S(1)}, u32[]{:S(2)}, u32[]{:S(2)}) collective-permute-start(f32[512,256]{1,0:T(8,128)S(1)} %get-tuple-element.337), channel_id=1, source_target_pairs={{0,7},{1,0},{2,1},{3,2},{4,3},{5,4},{6,5},{7,6},{8,15},{9,8},{10,9... | collective-permute-start | bytes 1572872 | tf_op jit(solution)/shard_map/while/body/eval_jaxpr/ppermute | solution.py:40
  197.8 8.2 %collective-permute-start = (f32[512,256]{1,0:T(8,128)S(1)}, f32[512,256]{1,0:T(8,128)S(1)}, u32[]{:S(2)}, u32[]{:S(2)}) collective-permute-start(f32[512,256]{1,0:T(8,128)S(1)} %get-tuple-element.337), channel_id=1, source_target_pairs={{0,7},{1,0},{2,1},{3,2},{4,3},{5,4},{6,5},{7,6},{8,15},{9,8},{10,9... | collective-permute-start | bytes 1572872 | tf_op jit(solution)/shard_map/while/body/eval_jaxpr/ppermute | solution.py:40
  214.0 8.2 %collective-permute-start = (f32[512,256]{1,0:T(8,128)S(1)}, f32[512,256]{1,0:T(8,128)S(1)}, u32[]{:S(2)}, u32[]{:S(2)}) collective-permute-start(f32[512,256]{1,0:T(8,128)S(1)} %get-tuple-element.337), channel_id=1, source_target_pairs={{0,7},{1,0},{2,1},{3,2},{4,3},{5,4},{6,5},{7,6},{8,15},{9,8},{10,9... | collective-permute-start | bytes 1572872 | tf_op jit(solution)/shard_map/while/body/eval_jaxpr/ppermute | solution.py:40
  228.5 11.6 %collective-permute-start = (f32[512,256]{1,0:T(8,128)S(1)}, f32[512,256]{1,0:T(8,128)S(1)}, u32[]{:S(2)}, u32[]{:S(2)}) collective-permute-start(f32[512,256]{1,0:T(8,128)S(1)} %get-tuple-element.337), channel_id=1, source_target_pairs={{0,7},{1,0},{2,1},{3,2},{4,3},{5,4},{6,5},{7,6},{8,15},{9,8},{10,9... | collective-permute-start | bytes 1572872 | tf_op jit(solution)/shard_map/while/body/eval_jaxpr/ppermute | solution.py:40
  246.4 11.6 %collective-permute-start = (f32[512,256]{1,0:T(8,128)S(1)}, f32[512,256]{1,0:T(8,128)S(1)}, u32[]{:S(2)}, u32[]{:S(2)}) collective-permute-start(f32[512,256]{1,0:T(8,128)S(1)} %get-tuple-element.337), channel_id=1, source_target_pairs={{0,7},{1,0},{2,1},{3,2},{4,3},{5,4},{6,5},{7,6},{8,15},{9,8},{10,9... | collective-permute-start | bytes 1572872 | tf_op jit(solution)/shard_map/while/body/eval_jaxpr/ppermute | solution.py:40
  264.4 11.6 %collective-permute-start = (f32[512,256]{1,0:T(8,128)S(1)}, f32[512,256]{1,0:T(8,128)S(1)}, u32[]{:S(2)}, u32[]{:S(2)}) collective-permute-start(f32[512,256]{1,0:T(8,128)S(1)} %get-tuple-element.337), channel_id=1, source_target_pairs={{0,7},{1,0},{2,1},{3,2},{4,3},{5,4},{6,5},{7,6},{8,15},{9,8},{10,9... | collective-permute-start | bytes 1572872 | tf_op jit(solution)/shard_map/while/body/eval_jaxpr/ppermute | solution.py:40
  276.0 0.8 copy-start
  276.0 1.0 copy-start.1
where the time goes:
time: 282 us; the launch traced here: 277 us
  waiting for transfers between devices  107 us (38%)
  starting transfers between devices  58 us (21%)
  local copies, waits for them, and re-layouts  45.1 us (16%)
  loops' own time  24.1 us (9%)
  other arithmetic  21.9 us (8%)
  matrix products  20.3 us (7%)
    ppermute x16, waiting for transfers between devices, sub_epoch(): return (user_new, lax.ppermute(item_new, 'shard', shift_perm))  107 us
    ppermute x16, starting transfers between devices, sub_epoch(): return (user_new, lax.ppermute(item_new, 'shard', shift_perm))  58 us
    another operation x16, loops' own time, sub_epoch(): lax.fori_loop(0, step_row[col_id], grad_step, (user_cur, item_cur))  23.1 us
    ne x16, other arithmetic, sub_epoch(): lax.dynamic_slice_in_dim(obs_mask, col_id * items_dev, items_dev, axis=1)  21.9 us
    dynamic_slice x16, local copies, waits for them, and re-layouts, sub_epoch(): lax.dynamic_slice_in_dim(ratings, col_id * items_dev, items_dev, axis=1)  20.8 us
    dynamic_slice x16, local copies, waits for them, and re-layouts, sub_epoch(): step_row[col_id]  20 us
    dot_general x20, matrix products, grad_step(): jnp.einsum('ur,ir->ui', user_half, item_half, preferred_element_type=jnp....  6.92 us
    dot_general x20, matrix products, grad_step(): jnp.einsum('ui,ur->ir', err_half, user_half, preferred_element_type=jnp.f...  6.83 us
  transfers between devices with their start and end apart: 16, of which 16 were waited for; matrix products, arithmetic and copies ran while one was open for 0% of the time, Pallas kernels for 0%

commit v1 on v0

v1 whole, which is shorter than its diff:
```python
import functools
import math
import jax
import jax.numpy as jnp
from jax import lax
from jax.experimental import pallas as pl
from jax.experimental.pallas import tpu as pltpu
from jax.sharding import PartitionSpec as P

EPOCHS = 2
CHUNKS = 2
ROWS = 256
F32 = jnp.float32
BF16 = jnp.bfloat16
MESH = pl.DeviceIdType.MESH


def dot_nn(lhs, rhs):
    return jnp.dot(lhs, rhs, preferred_element_type=F32)


def dot_nt(lhs, rhs):
    return lax.dot_general(lhs, rhs, (((1,), (1,)), ((), ())), preferred_element_type=F32)


def sgd_kernel(group, axis, steps_ref, user_ref, item_ref, ratings_ref, mask_ref, user_out, item_out,
               rate_v, seen_v, vin, vout, v_mid, user_v, user_h, user_t, grad_u, err_v,
               rate_sem, seen_sem, send_sem, recv_sem):
    users, rank = user_ref.shape
    items = item_ref.shape[0]
    width = items // CHUNKS
    levels = EPOCHS * group
    eta = 0.4 * math.sqrt(rank) / (users + rank)
    lam = 0.1 * items / math.sqrt(rank)
    me = lax.axis_index(axis)
    left = lax.rem(me + group - 1, group)
    right = lax.rem(me + 1, group)

    def load(sweep):
        col = lax.rem(me + sweep, group)
        src = pl.ds(pl.multiple_of(col * items, items), items)
        return (
            pltpu.make_async_copy(ratings_ref.at[:, src], rate_v.at[col], rate_sem.at[sweep]),
            pltpu.make_async_copy(mask_ref.at[:, src], seen_v.at[col], seen_sem.at[sweep]),
        )

    def hop(sweep, k):
        return pltpu.make_async_remote_copy(
            src_ref=vout.at[sweep, k],
            dst_ref=vin.at[sweep + 1, k],
            send_sem=send_sem.at[sweep, k],
            recv_sem=recv_sem.at[sweep, k],
            device_id={axis: left},
            device_id_type=MESH,
        )

    for sweep in range(group):
        for copy in load(sweep):
            copy.start()

    barrier = pltpu.get_barrier_semaphore()
    for other in (left, right):
        pl.semaphore_signal(barrier, inc=1, device_id={axis: other}, device_id_type=MESH)

    def put_user(value):
        user_v[...] = value
        half = value.astype(BF16)
        user_h[...] = half
        user_t[...] = half.T

    put_user(user_ref[...])
    for k in range(CHUNKS):
        vin[0, k] = item_ref[k * width:(k + 1) * width, :].T
    pl.semaphore_wait(barrier, 2)

    def grad_step(col, k, v_now):
        half = v_now.astype(BF16)
        for row in range(0, users, ROWS):
            rows = slice(row, row + ROWS)
            cols = slice(k * width, (k + 1) * width)
            approx = dot_nn(user_h[rows, :], half)
            err = jnp.where(seen_v[col, rows, cols] != 0, approx - rate_v[col, rows, cols], 0.0).astype(BF16)
            err_v[rows, :] = err
            part = dot_nt(err, half)
            if k == 0:
                grad_u[rows, :] = part
            else:
                grad_u[rows, :] += part
        grad_v = dot_nn(user_t[...], err_v[...])
        return v_now - eta * (grad_v + lam * v_now)

    def level(sweep, carry):
        col = lax.rem(me + sweep, group)
        twice = steps_ref[0, col] > 1

        @pl.when(sweep < group)
        def _():
            for copy in load(sweep):
                copy.wait()

        for k in range(CHUNKS):
            @pl.when(sweep > 0)
            def _():
                hop(sweep - 1, k).wait_recv()

            v_mid[k] = grad_step(col, k, vin[sweep, k])
        user_now = user_v[...]
        put_user(user_now - eta * (grad_u[...] + lam * user_now))
        for k in range(CHUNKS):
            v_now = v_mid[k]
            v_new = grad_step(col, k, v_now)
            vout[sweep, k] = jnp.where(twice, v_new, v_now)
            hop(sweep, k).start()
        user_now = user_v[...]
        user_new = user_now - eta * (grad_u[...] + lam * user_now)
        put_user(jnp.where(twice, user_new, user_now))
        return carry

    lax.fori_loop(0, levels, level, 0)

    user_out[...] = user_v[...]
    for k in range(CHUNKS):
        hop(levels - 1, k).wait_recv()
        item_out[k * width:(k + 1) * width, :] = vin[levels, k].T

    def drain(sweep, carry):
        for k in range(CHUNKS):
            hop(sweep, k).wait_send()
        return carry

    lax.fori_loop(0, levels, drain, 0)


def solution(mesh):
    axis = "shard"
    group = mesh.shape[axis]
    row_spec = P(("rep", axis), None)
    levels = EPOCHS * group

    def local_run(ratings, obs_mask, step_counts, user_init, item_init):
        users, rank = user_init.shape
        items = item_init.shape[0]
        width = items // CHUNKS
        vmem = pl.BlockSpec(memory_space=pltpu.VMEM)
        hbm = pl.BlockSpec(memory_space=pl.ANY)
        return pl.pallas_call(
            functools.partial(sgd_kernel, group, axis),
            name="sgd",
            out_shape=(
                jax.ShapeDtypeStruct((users, rank), F32),
                jax.ShapeDtypeStruct((items, rank), F32),
            ),
            in_specs=[pl.BlockSpec(memory_space=pltpu.SMEM), vmem, vmem, hbm, hbm],
            out_specs=(vmem, vmem),
            scratch_shapes=[
                pltpu.VMEM((group, users, items), F32),
                pltpu.VMEM((group, users, items), jnp.int32),
                pltpu.VMEM((levels + 1, CHUNKS, rank, width), F32),
                pltpu.VMEM((levels, CHUNKS, rank, width), F32),
                pltpu.VMEM((CHUNKS, rank, width), F32),
                pltpu.VMEM((users, rank), F32),
                pltpu.VMEM((users, rank), BF16),
                pltpu.VMEM((rank, users), BF16),
                pltpu.VMEM((users, rank), F32),
                pltpu.VMEM((users, width), BF16),
                pltpu.SemaphoreType.DMA((group,)),
                pltpu.SemaphoreType.DMA((group,)),
                pltpu.SemaphoreType.DMA((levels, CHUNKS)),
                pltpu.SemaphoreType.DMA((levels, CHUNKS)),
            ],
            compiler_params=pltpu.CompilerParams(
                collective_id=0, has_side_effects=True, vmem_limit_bytes=60 * 1024 * 1024
            ),
        )(step_counts, user_init, item_init, ratings, obs_mask)

    return jax.shard_map(local_run, mesh=mesh, in_specs=(row_spec,) * 5, out_specs=(row_spec, row_spec), check_vma=False)
```

time: 282 us -> 105 us (0.37)
  the two profiles are of different devices: /device:TPU:112 before, /device:TPU:113 now
where the time goes in v1:
time: 105 us
  Pallas kernels  100 us (95%)
  local copies, waits for them, and re-layouts  3.74 us (4%)
    pallas_call x1, Pallas kernels, local_run(): pl.pallas_call(functools.partial(sgd_kernel, group, axis), name='sgd', ou...  100 us
    unnamed x2, local copies, waits for them, and re-layouts  3.74 us

profile of v1, /device:TPU:113, one launch (start us, length us, event | category | flops | bytes accessed | tf_op | source)
XLA Modules:
  0.0 104.8 jit_solution(17390780649332381022)
XLA Ops:
  0.6 100.4 %sgd.1 = (f32[512,256]{1,0:T(8,128)}, f32[512,256]{1,0:T(8,128)}) custom-call(s32[1,8]{1,0:T(1,128)} %steps_ref.1, f32[512,256]{1,0:T(8,128)} %user_ref.1, f32[512,256]{1,0:T(8,128)} %item_ref.1, f32[512,4096]{1,0:T(8,128)} %ratings_ref.1, s32[512,4096]{1,0:T(8,128)} %mask_ref.1), custom_call_target="tpu_custom_call" | custom-call | tf_op jit(solution)/shard_map/sgd/pallas_call | solution.py:146
  101.0 1.9 %copy.9 = f32[512,256]{1,0:T(8,128)} copy(f32[512,256]{1,0:T(8,128)} %get-tuple-element.4) | data formatting | bytes 1048576
  102.9 1.9 %copy.10 = f32[512,256]{1,0:T(8,128)} copy(f32[512,256]{1,0:T(8,128)} %get-tuple-element.5) | data formatting | bytes 1048576

commit v2 on v1

--- a/solution.py
+++ b/solution.py
@@ -24,8 +24,8 @@
 
 
 def sgd_kernel(group, axis, steps_ref, user_ref, item_ref, ratings_ref, mask_ref, user_out, item_out,
-               rate_v, seen_v, vin, vout, v_mid, user_v, user_h, user_t, grad_u, err_v,
-               rate_sem, seen_sem, send_sem, recv_sem):
+               rate_v, seen_v, vin, vout, v_mid, item_v, user_v, user_h, user_t, grad_u, err_v,
+               rate_sem, seen_sem, send_sem, recv_sem, side_sem):
     users, rank = user_ref.shape
     items = item_ref.shape[0]
     width = items // CHUNKS
@@ -54,10 +54,10 @@
             device_id_type=MESH,
         )
 
-    for sweep in range(group):
-        for copy in load(sweep):
-            copy.start()
-
+    user_in = pltpu.make_async_copy(user_ref, user_v, side_sem.at[0])
+    item_in = pltpu.make_async_copy(item_ref, item_v, side_sem.at[1])
+    for copy in (user_in, item_in, *load(0)):
+        copy.start()
     barrier = pltpu.get_barrier_semaphore()
     for other in (left, right):
         pl.semaphore_signal(barrier, inc=1, device_id={axis: other}, device_id_type=MESH)
@@ -68,9 +68,11 @@
         user_h[...] = half
         user_t[...] = half.T
 
-    put_user(user_ref[...])
+    user_in.wait()
+    put_user(user_v[...])
+    item_in.wait()
     for k in range(CHUNKS):
-        vin[0, k] = item_ref[k * width:(k + 1) * width, :].T
+        vin[0, k] = item_v[k * width:(k + 1) * width, :].T
     pl.semaphore_wait(barrier, 2)
 
     def grad_step(col, k, v_now):
@@ -98,6 +100,11 @@
             for copy in load(sweep):
                 copy.wait()
 
+        @pl.when(sweep + 1 < group)
+        def _():
+            for copy in load(sweep + 1):
+                copy.start()
+
         for k in range(CHUNKS):
             @pl.when(sweep > 0)
             def _():
@@ -131,6 +138,17 @@
     lax.fori_loop(0, levels, drain, 0)
 
 
+def emit_kernel(user_v, item_v, user_out, item_out, sem):
+    copies = (
+        pltpu.make_async_copy(user_v, user_out, sem.at[0]),
+        pltpu.make_async_copy(item_v, item_out, sem.at[1]),
+    )
+    for copy in copies:
+        copy.start()
+    for copy in copies:
+        copy.wait()
+
+
 def solution(mesh):
     axis = "shard"
     group = mesh.shape[axis]
@@ -143,14 +161,14 @@
         width = items // CHUNKS
         vmem = pl.BlockSpec(memory_space=pltpu.VMEM)
         hbm = pl.BlockSpec(memory_space=pl.ANY)
-        return pl.pallas_call(
+        user_new, item_new = pl.pallas_call(
             functools.partial(sgd_kernel, group, axis),
             name="sgd",
             out_shape=(
-                jax.ShapeDtypeStruct((users, rank), F32),
-                jax.ShapeDtypeStruct((items, rank), F32),
+                pltpu.VMEM((users, rank), F32),
+                pltpu.VMEM((items, rank), F32),
             ),
-            in_specs=[pl.BlockSpec(memory_space=pltpu.SMEM), vmem, vmem, hbm, hbm],
+            in_specs=[pl.BlockSpec(memory_space=pltpu.SMEM), hbm, hbm, hbm, hbm],
             out_specs=(vmem, vmem),
             scratch_shapes=[
                 pltpu.VMEM((group, users, items), F32),
@@ -158,6 +176,7 @@
                 pltpu.VMEM((levels + 1, CHUNKS, rank, width), F32),
                 pltpu.VMEM((levels, CHUNKS, rank, width), F32),
                 pltpu.VMEM((CHUNKS, rank, width), F32),
+                pltpu.VMEM((items, rank), F32),
                 pltpu.VMEM((users, rank), F32),
                 pltpu.VMEM((users, rank), BF16),
                 pltpu.VMEM((rank, users), BF16),
@@ -167,10 +186,22 @@
                 pltpu.SemaphoreType.DMA((group,)),
                 pltpu.SemaphoreType.DMA((levels, CHUNKS)),
                 pltpu.SemaphoreType.DMA((levels, CHUNKS)),
+                pltpu.SemaphoreType.DMA((2,)),
             ],
             compiler_params=pltpu.CompilerParams(
                 collective_id=0, has_side_effects=True, vmem_limit_bytes=60 * 1024 * 1024
             ),
         )(step_counts, user_init, item_init, ratings, obs_mask)
+        return pl.pallas_call(
+            emit_kernel,
+            name="emit",
+            out_shape=(
+                jax.ShapeDtypeStruct((users, rank), F32),
+                jax.ShapeDtypeStruct((items, rank), F32),
+            ),
+            in_specs=[vmem, vmem],
+            out_specs=(hbm, hbm),
+            scratch_shapes=[pltpu.SemaphoreType.DMA((2,))],
+        )(*(pltpu.with_memory_space_constraint(x, pltpu.VMEM) for x in (user_new, item_new)))
 
     return jax.shard_map(local_run, mesh=mesh, in_specs=(row_spec,) * 5, out_specs=(row_spec, row_spec), check_vma=False)

time: 105 us -> 101 us (0.962)
  local copies, waits for them, and re-layouts: 3.74 us -> 0 us
    unnamed x2 -> x0, local copies, waits for them, and re-layouts: 3.74 us -> none
    pallas_call x1, Pallas kernels: 100 us -> 99.1 us  [local_run(): pl.pallas_call(functools.partial(sgd_kernel, group, axis), name='sgd', ou...]
where the time goes in v2:
time: 101 us
  Pallas kernels  100 us (99%)
    pallas_call x1, Pallas kernels, local_run(): pl.pallas_call(functools.partial(sgd_kernel, group, axis), name='sgd', ou...  99.1 us

profile of v2, /device:TPU:113, one launch (start us, length us, event | category | flops | bytes accessed | tf_op | source)
XLA Modules:
  0.0 100.7 jit_solution(15277601335314810034)
XLA Ops:
  0.6 99.1 %sgd.1 = (f32[512,256]{1,0:T(8,128)S(1)}, f32[512,256]{1,0:T(8,128)S(1)}) custom-call(s32[1,8]{1,0:T(1,128)} %steps_ref.1, f32[512,256]{1,0:T(8,128)} %user_ref.1, f32[512,256]{1,0:T(8,128)} %item_ref.1, f32[512,4096]{1,0:T(8,128)} %ratings_ref.1, s32[512,4096]{1,0:T(8,128)} %mask_ref.1), custom_call_target="tpu_custom_call" | custom-call | tf_op jit(solution)/shard_map/sgd/pallas_call | solution.py:164
  99.8 1.0 emit.1
